TPU v7x, 32 devices: a whole 2x2x4 slice. The times are simulated.
32 devices in a mesh: grp: 2 (over y), tile: 4 (over z), coil: 2 (over x), spk: 2 (over core).
Axes of the slice: x: 2, y: 2, z: 4, core: 2. Of those that a mesh axis runs over, the one named last changes fastest.
Arguments:
- coil_maps: float32 [2, 512, 2, 256], P('coil', ('grp', 'tile', 'spk')), parts along dimension 1, may hold values from -6 to 6
- kspace_data: bfloat16 [2, 128, 2, 256], P('coil', ('grp', 'tile', 'spk')), parts along dimension 1, may hold values from -24 to 24
- interp_weights: bfloat16 [128, 6, 256], P(('grp', 'tile', 'spk')), parts along dimension 0, may hold values from 0.099609375 to 1
- sample_bins: int32 [128, 256], P(('grp', 'tile', 'spk')), parts along dimension 0, may hold values from 0 to 65535, as said below
- spoke_count: int32 [16], P(('grp', 'tile', 'spk')), parts along dimension 0, may hold values from 1 to 8, 32 in all
- thresholds: float32 [3], replicated, may hold values from 0.05 to 0.3
Outputs:
- image: float32 [512, 2, 256], P(('grp', 'tile', 'spk')), parts along dimension 0
There are 2 independent parts, one for each index of `grp`. A program takes and returns all parts, laid end to end along the dimension named above; an argument that names none is the same for every part. Nothing has to cross between parts.
Inputs may be any that keep to these rules, and one draw needn't show every extreme that they name: `sample_bins`: sample k of each spoke lies on a straight line through cell (128, 128), at offset k - 128 along the spoke's direction, coordinates taken modulo 256. `spoke_count`: each independent slice has its own 8 counts, and the whole array holds one such block of counts per slice. The 8 counts of each slice sum to 32. In every draw, at least one device of each slice holds 8 live spokes. A device's live spokes are its first ones.
All inputs are finite; a program needn't handle non-finite values.
Results may differ from a plain program's by a relative error of at most 0.0016.
Values may be sent and summed in bfloat16 or wider, within the bound.
A program may use at most 64 MiB of HBM per device.

v0:
```python
import math
import jax
import jax.numpy as jnp
from jax import lax
from jax.sharding import PartitionSpec as P

N = 256
RO = 256
SPK_DEV = 8
LEVELS = 3
ITERS = 4
HIGH = lax.Precision.HIGHEST
STEP_SIZE = 0.5
RSQRT2 = 0.7071067811865476


def dft_table(length, direction):
    positions = jnp.arange(length, dtype=jnp.int32)
    phases = positions[:, None] * positions[None, :] % length
    angles = phases.astype(jnp.float32) * jnp.float32(2.0 * math.pi / length)
    norm_scale = 1.0 / math.sqrt(length)
    cosine = jnp.cos(angles) * norm_scale
    sine_tab = jnp.sin(angles) * norm_scale
    top_rows = jnp.stack([cosine, -direction * sine_tab], axis=1)
    bottom = jnp.stack([direction * sine_tab, cosine], axis=1)
    return jnp.stack([top_rows, bottom], axis=0)


def haar_matrix(length, levels):
    haar_mat = jnp.eye(length, dtype=jnp.float32)
    positions = jnp.arange(length, dtype=jnp.int32)
    out_i = positions[:, None]
    in_j = positions[None, :]
    for level_num in range(levels):
        span_len = length >> level_num
        half_len = span_len // 2
        low_hit = (out_i < half_len) & ((in_j == 2 * out_i) | (in_j == 2 * out_i + 1))
        high_pos = out_i - half_len
        high_hit = (
            (out_i >= half_len)
            & (out_i < span_len)
            & ((in_j == 2 * high_pos) | (in_j == 2 * high_pos + 1))
        )
        sign_val = jnp.where(in_j == 2 * high_pos + 1, -1.0, 1.0)
        step_mat = jnp.where(low_hit, RSQRT2, jnp.where(high_hit, sign_val * RSQRT2, 0.0))
        step_mat = step_mat + jnp.where((out_i >= span_len) & (in_j == out_i), 1.0, 0.0)
        haar_mat = jnp.dot(step_mat.astype(jnp.float32), haar_mat, precision=HIGH)
    return haar_mat


def haar_labels(length, levels):
    positions = jnp.arange(length, dtype=jnp.int32)
    band_label = jnp.ones((length,), jnp.int32)
    for level_num in range(1, levels + 1):
        band_label = band_label + (positions < length >> level_num).astype(jnp.int32)
    return band_label


def wavelet_shrink(target, thresholds, levels):
    row_count, pair_dim, col_count = target.shape
    block_len = 2**levels
    row_haar = haar_matrix(block_len, levels)
    col_haar = haar_matrix(col_count, levels)
    grouped = target.reshape(row_count // block_len, block_len, pair_dim, col_count)
    coeffs = jnp.einsum("ij,gjpc->gipc", row_haar, grouped, precision=HIGH)
    coeffs = jnp.einsum("gipc,kc->gipk", coeffs, col_haar, precision=HIGH)
    band_min = jnp.minimum(
        haar_labels(block_len, levels)[:, None], haar_labels(col_count, levels)[None, :]
    )
    active = band_min <= levels
    limits = jnp.ones(band_min.shape, jnp.float32)
    for level_num in range(levels):
        limits = jnp.where(band_min == level_num + 1, thresholds[level_num], limits)
    magnitude = jnp.sqrt(coeffs[:, :, 0] ** 2 + coeffs[:, :, 1] ** 2)
    factor = jnp.maximum(magnitude - limits, 0.0) / jnp.maximum(magnitude, limits)
    factor = jnp.where(active, factor, 1.0)
    shrunk = coeffs * factor[:, :, None, :]
    restored = jnp.einsum("gipk,kc->gipc", shrunk, col_haar, precision=HIGH)
    restored = jnp.einsum("ij,gipc->gjpc", row_haar, restored, precision=HIGH)
    return restored.reshape(row_count, pair_dim, col_count)


def complex_mul(left, right):
    real_part = left[:, 0] * right[:, 0] - left[:, 1] * right[:, 1]
    imag_part = left[:, 0] * right[:, 1] + left[:, 1] * right[:, 0]
    return jnp.stack([real_part, imag_part], axis=1)


def conj_mul(left, right):
    real_part = left[:, 0] * right[:, 0] + left[:, 1] * right[:, 1]
    imag_part = left[:, 0] * right[:, 1] - left[:, 1] * right[:, 0]
    return jnp.stack([real_part, imag_part], axis=1)


def interp_tables(load_bins, load_interp):
    grid_ids = jnp.arange(N, dtype=jnp.int32)
    row_bins = load_bins // N
    col_bins = load_bins % N
    zero_val = jnp.zeros((), jnp.bfloat16)
    row_table = jnp.zeros((load_bins.shape[0], load_bins.shape[1], N), jnp.bfloat16)
    col_table = jnp.zeros((load_bins.shape[0], N, load_bins.shape[1]), jnp.bfloat16)
    for tap_index in range(3):
        row_hit = grid_ids[None, None, :] == ((row_bins + tap_index - 1) % N)[:, :, None]
        row_table = row_table + jnp.where(
            row_hit, load_interp[:, tap_index, :][:, :, None], zero_val
        )
        col_hit = grid_ids[None, :, None] == ((col_bins + tap_index - 1) % N)[:, None, :]
        col_table = col_table + jnp.where(
            col_hit, load_interp[:, 3 + tap_index, :][:, None, :], zero_val
        )
    return (row_table, col_table)


def local(coil_maps, kspace_data, interp_weights, sample_bins, spoke_count, thresholds):
    blocks = lax.axis_size(("tile", "spk"))
    row_count = coil_maps.shape[1]
    live_total = blocks * SPK_DEV // 2
    coil_sens = coil_maps[0]
    measured = kspace_data[0]
    my_index = lax.axis_index(("tile", "spk"))
    counts = lax.all_gather(spoke_count, ("tile", "spk"), axis=0, tiled=True)
    prefix = jnp.cumsum(counts) - counts
    per_peer = -(-SPK_DEV // blocks)
    peer_ids = jnp.arange(blocks, dtype=jnp.int32)
    first_slot = (peer_ids - prefix[my_index]) % blocks
    slot_index = first_slot[:, None] + blocks * jnp.arange(per_peer, dtype=jnp.int32)[None, :]
    picked = jnp.clip(slot_index, 0, SPK_DEV - 1)
    values = jnp.concatenate([measured, interp_weights], axis=1)
    got_values = lax.all_to_all(
        values[picked], ("tile", "spk"), split_axis=0, concat_axis=0, tiled=True
    )
    got_bins = lax.all_to_all(
        sample_bins[picked], ("tile", "spk"), split_axis=0, concat_axis=0, tiled=True
    )
    my_share = SPK_DEV // 2
    wanted = my_index + blocks * jnp.arange(my_share, dtype=jnp.int32)
    source = jnp.sum((prefix[None, :] <= wanted[:, None]).astype(jnp.int32), axis=1) - 1
    depth_at = (wanted - prefix[source]) // blocks
    loaded = got_values[source, depth_at]
    load_bins = got_bins[source, depth_at]
    load_data = loaded[:, 0:2]
    load_interp = loaded[:, 2:8]
    row_table, col_table = interp_tables(load_bins, load_interp)
    n_load = row_table.shape[0]
    offset = jnp.abs(jnp.arange(RO, dtype=jnp.int32) - RO // 2).astype(jnp.float32)
    density = (offset + 0.5) * (N / (3.0 * RO * live_total))
    target_data = load_data.astype(jnp.float32)
    fwd_table = dft_table(N, 1.0)
    inv_table = dft_table(N, -1.0)

    def grid_rows(weighted):

        def grid_term(row_start, piece_rows):

            def grid_one_spoke(spoke_index, partial_value):
                row_one = lax.dynamic_index_in_dim(row_table, spoke_index, 0, keepdims=False)
                col_one = lax.dynamic_index_in_dim(col_table, spoke_index, 0, keepdims=False)
                col_slice = col_one.astype(jnp.float32)
                residue = lax.dynamic_index_in_dim(weighted, spoke_index, 0, keepdims=False)
                smeared = (col_slice[:, None, :] * residue[None, :, :]).astype(jnp.bfloat16)
                added = jnp.dot(
                    smeared.reshape(piece_rows * 2, RO), row_one, preferred_element_type=jnp.float32
                )
                return partial_value + added.reshape(piece_rows, 2, N)

            return lax.fori_loop(
                0, my_share, grid_one_spoke, jnp.zeros((piece_rows, 2, N), jnp.float32)
            )

        return grid_term

    estimate = jnp.zeros((row_count, 2, N), jnp.float32)
    for iteration in range(ITERS):
        if iteration == 0:
            weighted = -density[None, None, :] * target_data
        else:
            coil_image = complex_mul(coil_sens, estimate)
            half_done = jnp.einsum("rpc,pcqv->rqv", coil_image, fwd_table, precision=HIGH)
            turned = lax.all_to_all(
                half_done, ("tile", "spk"), split_axis=2, concat_axis=0, tiled=True
            )
            kspace = jnp.einsum("rpv,prqu->vqu", turned, fwd_table, precision=HIGH).astype(
                jnp.bfloat16
            )
            piece = lax.all_gather(kspace, ("tile", "spk"), axis=0, tiled=True)
            fold_piece_rows = piece.shape[0]
            flat_piece = piece.reshape(fold_piece_rows * 2, N)

            def fold_one_spoke(spoke_index, partial_value):
                row_one = lax.dynamic_index_in_dim(row_table, spoke_index, 0, keepdims=False)
                col_one = lax.dynamic_index_in_dim(col_table, spoke_index, 0, keepdims=False)
                inner_sum = lax.dot_general(
                    flat_piece,
                    row_one,
                    (((1,), (1,)), ((), ())),
                    preferred_element_type=jnp.float32,
                )
                inner_sum = inner_sum.reshape(fold_piece_rows, 2, RO)
                col_slice = col_one.astype(jnp.float32)
                added = jnp.sum(inner_sum * col_slice[:, None, :], axis=0)
                current = lax.dynamic_index_in_dim(partial_value, spoke_index, 0, keepdims=False)
                return lax.dynamic_update_index_in_dim(
                    partial_value, current + added, spoke_index, 0
                )

            sample_model = lax.fori_loop(
                0, my_share, fold_one_spoke, jnp.zeros((n_load, 2, RO), jnp.float32)
            )
            weighted = density[None, None, :] * (sample_model - target_data)
        grid_term = grid_rows(weighted)
        owned_rows = lax.psum_scatter(
            grid_term(jnp.int32(0), row_count * lax.axis_size(("tile", "spk"))),
            ("tile", "spk"),
            scatter_dimension=0,
            tiled=True,
        )
        partial_back = jnp.einsum("vpu,puqr->vqr", owned_rows, inv_table, precision=HIGH)
        returned = lax.all_to_all(
            partial_back, ("tile", "spk"), split_axis=2, concat_axis=0, tiled=True
        )
        coil_back = jnp.einsum("vpr,pvqc->rqc", returned, inv_table, precision=HIGH)
        gradient = lax.psum(conj_mul(coil_sens, coil_back), "coil")
        estimate = wavelet_shrink(estimate - STEP_SIZE * gradient, thresholds, LEVELS)
    return estimate


def solution(mesh):
    placed = (
        P("coil", ("grp", "tile", "spk"), None, None),
        P("coil", ("grp", "tile", "spk"), None, None),
        P(("grp", "tile", "spk"), None, None),
        P(("grp", "tile", "spk"), None),
        P(("grp", "tile", "spk")),
        P(),
    )
    return jax.shard_map(
        local,
        mesh=mesh,
        in_specs=placed,
        out_specs=P(("grp", "tile", "spk"), None, None),
        check_vma=False,
    )
```

profile of v0, /device:TPU:0, one launch (start us, length us, event | category | flops | bytes accessed | tf_op | source)
XLA Modules:
  0.0 512.3 jit_solution(6684872715194408570)
XLA Ops:
  9.2 10.6 %all-reduce = s32[8]{0:T(128)S(1)} all-reduce(s32[8]{0:T(128)S(1)} %dynamic-update-slice), channel_id=1, replica_groups=mesh['grp'=2,'tile'=4,'coil'=2,'spk'=2] {'tile','spk'}, use_global_device_ids=true, to_apply=%add | all-reduce | flops 8 | bytes 64
  22.5 3.3 all-to-all-start
  34.2 5.0 all-to-all-start.1
  39.9 5.1 all-to-all-done.1
  47.7 7.5 %while.98 = (s32[]{:T(128)}, f32[256,2,256]{2,0,1:T(8,128)}, bf16[4,256,256]{2,1,0:T(8,128)(2,1)S(1)}, f32[4,2,256]{2,1,0:T(2,128)S(1)}, bf16[4,256,256]{2,1,0:T(8,128)(2,1)S(1)}, /*index=5*/s32[]{:T(128)}, s32[]{:T(128)}) while((s32[]{:T(128)}, f32[256,2,256]{2,0,1:T(8,128)}, bf16[4,256,256]{2,1,0:T(8,128)(2,1)S(1)}, ...), condition=%wide.region_3.4_spmd.clone, body=%wide.region_2.3_spmd.clone.sunk | while | flops 67698688 | bytes 1841251 | solution.py:166
  48.8 2.1 convolution_add_fusion.8
  51.0 2.1 convolution_add_fusion.8
  53.1 2.1 convolution_add_fusion.8
  57.0 2.7 select_select_fusion
  60.5 24.4 %reduce-scatter.5.cloned.1.call-done = f32[32,2,256]{2,0,1:T(8,128)} async-done(((f32[256,2,256]{2,0,1:T(8,128)}), f32[32,2,256]{2,0,1:T(8,128)}) %reduce-scatter.5.cloned.1.call-update) | async-done | bytes 65552 | tf_op jit(solution)/shard_map/reduce_scatter | solution.py:211
  89.2 3.4 all-to-all-start.2
  94.6 3.8 all-to-all-done.2
  107.4 18.6 %all-reduce.6.cloned.1.call-done = f32[32,2,256]{2,0,1:T(8,128)} async-done(((f32[32,2,256]{2,0,1:T(8,128)}), f32[32,2,256]{2,0,1:T(8,128)}) %all-reduce.6.cloned.1.call-update) | async-done | bytes 65552 | tf_op jit(solution)/shard_map/psum | solution.py:222
  133.2 4.6 all-to-all-start.3
  138.6 5.2 %all-to-all-done.3 = f32[8,1,2048]{2,1,0:T(1,128)} async-done(((f32[8,1,2048]{2,1,0:T(1,128)}), f32[8,1,2048]{2,1,0:T(1,128)}, u32[]{:S(2)}, u32[]{:S(2)}) %all-to-all-start.3) | async-done | bytes 65568 | tf_op jit(solution)/shard_map/all_to_all | solution.py:179
  143.8 2.2 reduce.1
  152.9 14.2 %all_gather.13 = bf16[256,2,256]{2,0,1:T(8,128)(2,1)S(1)} all-gather(bf16[32,2,256]{2,0,1:T(8,128)(2,1)S(1)} %fusion.32), channel_id=1, replica_groups=mesh['grp'=2,'tile'=4,'coil'=2,'spk'=2] {'tile','spk'}, dimensions={0}, use_global_device_ids=true | all-gather | bytes 294912 | tf_op jit(solution)/shard_map/all_gather | solution.py:185
  168.1 12.7 %while.95 = (s32[]{:T(128)}, f32[4,2,256]{2,1,0:T(2,128)}, bf16[4,256,256]{2,1,0:T(8,128)(2,1)S(1)}, bf16[512,256]{1,0:T(8,128)(2,1)S(1)}, bf16[4,256,256]{2,1,0:T(8,128)(2,1)S(1)}, /*index=5*/s32[]{:T(128)}) while((s32[]{:T(128)}, f32[4,2,256]{2,1,0:T(2,128)}, bf16[4,256,256]{2,1,0:T(8,128)(2,1)S(1)}, bf16[512,256]{1,0:T(8,128)(2,1)S(1)}, ...), condition=%wide.region_8.9_spmd, body=%wide.region_6.8_spmd.sunk | while | flops 67436544 | bytes 6300293 | solution.py:206
  182.3 7.5 %while.99 = (s32[]{:T(128)}, f32[256,2,256]{2,0,1:T(8,128)}, bf16[4,256,256]{2,1,0:T(8,128)(2,1)S(1)}, f32[4,2,256]{2,1,0:T(2,128)S(1)}, bf16[4,256,256]{2,1,0:T(8,128)(2,1)S(1)}, /*index=5*/s32[]{:T(128)}, s32[]{:T(128)}) while((s32[]{:T(128)}, f32[256,2,256]{2,0,1:T(8,128)}, bf16[4,256,256]{2,1,0:T(8,128)(2,1)S(1)}, ...), condition=%wide.region_10.11_spmd.clone, body=%wide.region_9.10_spmd.clone.sunk | while | flops 67698688 | bytes 1841251 | solution.py:166
  183.4 2.1 convolution_add_fusion.9
  185.5 2.1 convolution_add_fusion.9
  187.6 2.1 convolution_add_fusion.9
  189.8 28.9 %reduce-scatter.7.cloned.1.call-done = f32[32,2,256]{2,0,1:T(8,128)} async-done(((f32[256,2,256]{2,0,1:T(8,128)}), f32[32,2,256]{2,0,1:T(8,128)}) %reduce-scatter.7.cloned.1.call-update) | async-done | bytes 65552 | tf_op jit(solution)/shard_map/reduce_scatter | solution.py:211
  220.7 8.3 %all_to_all.136 = f32[8,1,2048]{2,1,0:T(1,128)S(1)} all-to-all(f32[8,1,2048]{2,1,0:T(1,128)S(1)} %reshape.884), channel_id=1, replica_groups=mesh['grp'=2,'tile'=4,'coil'=2,'spk'=2] {'tile','spk'}, dimensions={0} | all-to-all | bytes 131072 | tf_op jit(solution)/shard_map/all_to_all | solution.py:218
  231.7 19.7 %all-reduce.8.cloned.1.call-done = f32[32,2,256]{2,0,1:T(8,128)} async-done(((f32[32,2,256]{2,0,1:T(8,128)}), f32[32,2,256]{2,0,1:T(8,128)}) %all-reduce.8.cloned.1.call-update) | async-done | bytes 65552 | tf_op jit(solution)/shard_map/psum | solution.py:222
  258.9 4.6 all-to-all-start.5
  263.5 6.0 %all-to-all-done.5 = f32[8,1,2048]{2,1,0:T(1,128)} async-done(((f32[8,1,2048]{2,1,0:T(1,128)}), f32[8,1,2048]{2,1,0:T(1,128)}, u32[]{:S(2)}, u32[]{:S(2)}) %all-to-all-start.5) | async-done | bytes 65568 | tf_op jit(solution)/shard_map/all_to_all | solution.py:179
  269.5 2.2 reduce.3
  278.6 14.2 %all_gather.14 = bf16[256,2,256]{2,0,1:T(8,128)(2,1)S(1)} all-gather(bf16[32,2,256]{2,0,1:T(8,128)(2,1)S(1)} %fusion.33), channel_id=1, replica_groups=mesh['grp'=2,'tile'=4,'coil'=2,'spk'=2] {'tile','spk'}, dimensions={0}, use_global_device_ids=true | all-gather | bytes 294912 | tf_op jit(solution)/shard_map/all_gather | solution.py:185
  293.8 12.7 %while.96 = (s32[]{:T(128)}, f32[4,2,256]{2,1,0:T(2,128)}, bf16[4,256,256]{2,1,0:T(8,128)(2,1)S(1)}, bf16[512,256]{1,0:T(8,128)(2,1)S(1)}, bf16[4,256,256]{2,1,0:T(8,128)(2,1)S(1)}, /*index=5*/s32[]{:T(128)}) while((s32[]{:T(128)}, f32[4,2,256]{2,1,0:T(2,128)}, bf16[4,256,256]{2,1,0:T(8,128)(2,1)S(1)}, bf16[512,256]{1,0:T(8,128)(2,1)S(1)}, ...), condition=%wide.region_15.16_spmd, body=%wide.region_13.15_spmd.sunk | while | flops 67436544 | bytes 6300293 | solution.py:206
  307.9 7.5 %while.100 = (s32[]{:T(128)}, f32[256,2,256]{2,0,1:T(8,128)}, bf16[4,256,256]{2,1,0:T(8,128)(2,1)S(1)}, f32[4,2,256]{2,1,0:T(2,128)S(1)}, bf16[4,256,256]{2,1,0:T(8,128)(2,1)S(1)}, /*index=5*/s32[]{:T(128)}, s32[]{:T(128)}) while((s32[]{:T(128)}, f32[256,2,256]{2,0,1:T(8,128)}, bf16[4,256,256]{2,1,0:T(8,128)(2,1)S(1)}, ...), condition=%wide.region_17.18_spmd.clone, body=%wide.region_16.17_spmd.clone.sunk | while | flops 67698688 | bytes 1841251 | solution.py:166
  309.0 2.1 convolution_add_fusion.10
  311.1 2.1 convolution_add_fusion.10
  315.6 28.8 %reduce-scatter.9.cloned.1.call-done = f32[32,2,256]{2,0,1:T(8,128)} async-done(((f32[256,2,256]{2,0,1:T(8,128)}), f32[32,2,256]{2,0,1:T(8,128)}) %reduce-scatter.9.cloned.1.call-update) | async-done | bytes 65552 | tf_op jit(solution)/shard_map/reduce_scatter | solution.py:211
  346.4 8.3 %all_to_all.137 = f32[8,1,2048]{2,1,0:T(1,128)S(1)} all-to-all(f32[8,1,2048]{2,1,0:T(1,128)S(1)} %reshape.888), channel_id=1, replica_groups=mesh['grp'=2,'tile'=4,'coil'=2,'spk'=2] {'tile','spk'}, dimensions={0} | all-to-all | bytes 131072 | tf_op jit(solution)/shard_map/all_to_all | solution.py:218
  357.4 19.5 %all-reduce.10.cloned.1.call-done = f32[32,2,256]{2,0,1:T(8,128)} async-done(((f32[32,2,256]{2,0,1:T(8,128)}), f32[32,2,256]{2,0,1:T(8,128)}) %all-reduce.10.cloned.1.call-update) | async-done | bytes 65552 | tf_op jit(solution)/shard_map/psum | solution.py:222
  384.4 4.6 all-to-all-start.7
  389.0 6.0 %all-to-all-done.7 = f32[8,1,2048]{2,1,0:T(1,128)} async-done(((f32[8,1,2048]{2,1,0:T(1,128)}), f32[8,1,2048]{2,1,0:T(1,128)}, u32[]{:S(2)}, u32[]{:S(2)}) %all-to-all-start.7) | async-done | bytes 65568 | tf_op jit(solution)/shard_map/all_to_all | solution.py:179
  395.0 2.2 reduce.5
  404.1 14.2 %all_gather.15 = bf16[256,2,256]{2,0,1:T(8,128)(2,1)S(1)} all-gather(bf16[32,2,256]{2,0,1:T(8,128)(2,1)S(1)} %fusion.34), channel_id=1, replica_groups=mesh['grp'=2,'tile'=4,'coil'=2,'spk'=2] {'tile','spk'}, dimensions={0}, use_global_device_ids=true | all-gather | bytes 294912 | tf_op jit(solution)/shard_map/all_gather | solution.py:185
  419.3 12.7 %while.97 = (s32[]{:T(128)}, f32[4,2,256]{2,1,0:T(2,128)}, bf16[4,256,256]{2,1,0:T(8,128)(2,1)S(1)}, bf16[512,256]{1,0:T(8,128)(2,1)S(1)}, bf16[4,256,256]{2,1,0:T(8,128)(2,1)S(1)}, /*index=5*/s32[]{:T(128)}) while((s32[]{:T(128)}, f32[4,2,256]{2,1,0:T(2,128)}, bf16[4,256,256]{2,1,0:T(8,128)(2,1)S(1)}, bf16[512,256]{1,0:T(8,128)(2,1)S(1)}, ...), condition=%wide.region_22.23_spmd, body=%wide.region_20.22_spmd.sunk | while | flops 67436544 | bytes 6300293 | solution.py:206
  433.5 7.5 %while.101 = (s32[]{:T(128)}, f32[256,2,256]{2,0,1:T(8,128)}, bf16[4,256,256]{2,1,0:T(8,128)(2,1)S(1)}, f32[4,2,256]{2,1,0:T(2,128)S(1)}, bf16[4,256,256]{2,1,0:T(8,128)(2,1)S(1)}, /*index=5*/s32[]{:T(128)}, s32[]{:T(128)}) while((s32[]{:T(128)}, f32[256,2,256]{2,0,1:T(8,128)}, bf16[4,256,256]{2,1,0:T(8,128)(2,1)S(1)}, ...), condition=%wide.region_24.25_spmd.clone, body=%wide.region_23.24_spmd.clone.sunk | while | flops 67698688 | bytes 1841251 | solution.py:166
  434.6 2.1 convolution_add_fusion.11
  436.7 2.1 convolution_add_fusion.11
  438.9 2.1 convolution_add_fusion.11
  441.0 28.9 %reduce-scatter.11.cloned.1.call-done = f32[32,2,256]{2,0,1:T(8,128)} async-done(((f32[256,2,256]{2,0,1:T(8,128)}), f32[32,2,256]{2,0,1:T(8,128)}) %reduce-scatter.11.cloned.1.call-update) | async-done | bytes 65552 | tf_op jit(solution)/shard_map/reduce_scatter | solution.py:211
  472.0 8.3 %all_to_all.138 = f32[8,1,2048]{2,1,0:T(1,128)S(1)} all-to-all(f32[8,1,2048]{2,1,0:T(1,128)S(1)} %reshape.892), channel_id=1, replica_groups=mesh['grp'=2,'tile'=4,'coil'=2,'spk'=2] {'tile','spk'}, dimensions={0} | all-to-all | bytes 131072 | tf_op jit(solution)/shard_map/all_to_all | solution.py:218
  483.0 19.5 %all-reduce.12.cloned.1.call-done = f32[32,2,256]{2,0,1:T(8,128)} async-done(((f32[32,2,256]{2,0,1:T(8,128)}), f32[32,2,256]{2,0,1:T(8,128)}) %all-reduce.12.cloned.1.call-update) | async-done | bytes 65552 | tf_op jit(solution)/shard_map/psum | solution.py:222
  (406 shorter events, 145.9 us)
Async XLA Ops:
  6.5 14.8 %copy-start = (s32[8,256]{1,0:T(8,128)S(1)}, s32[8,256]{1,0:T(8,128)}, u32[]{:S(2)}) copy-start(s32[8,256]{1,0:T(8,128)} %param.23) | copy-start | bytes 24580
  22.5 11.7 %all-to-all-start = ((s32[8,1,256]{2,1,0:T(1,128)}), s32[8,1,256]{2,1,0:T(1,128)S(1)}, u32[]{:S(2)}, u32[]{:S(2)}) async-start(s32[8,1,256]{2,1,0:T(1,128)} %copy.115), calls=%async_computation | async-start | bytes 16384 | tf_op jit(solution)/shard_map/all_to_all | solution.py:132
  27.9 31.9 %copy-start.26 = (s32[8]{0:T(128)}, s32[8]{0:T(128)S(1)}, u32[]{:S(2)}) copy-start(s32[8]{0:T(128)S(1)} %get-tuple-element.881) | copy-start | bytes 100
  27.9 31.9 %copy-start.28 = (s32[8]{0:T(128)}, s32[8]{0:T(128)S(1)}, u32[]{:S(2)}) copy-start(s32[8]{0:T(128)S(1)} %get-tuple-element.882) | copy-start | bytes 100
  28.9 0.7 copy-start.19
  29.7 1.3 copy-start.23
  31.2 120.2 %copy-start.1 = (f32[1,256,2,256]{3,1,2,0:T(8,128)}, f32[1,256,2,256]{3,1,2,0:T(8,128)S(1)}, u32[]{:S(2)}) copy-start(f32[1,256,2,256]{3,1,2,0:T(8,128)S(1)} %get-tuple-element.830) | copy-start | bytes 1572868
  31.2 120.2 %copy-start.4 = (f32[1,256,2,256]{3,1,2,0:T(8,128)}, f32[1,256,2,256]{3,1,2,0:T(8,128)S(1)}, u32[]{:S(2)}) copy-start(f32[1,256,2,256]{3,1,2,0:T(8,128)S(1)} %get-tuple-element.833) | copy-start | bytes 1572868
  34.2 10.8 %all-to-all-start.1 = ((bf16[8,1,8,256]{3,2,1,0:T(8,128)(2,1)}), bf16[8,1,8,256]{3,2,1,0:T(8,128)(2,1)S(1)}, u32[]{:S(2)}, u32[]{:S(2)}) async-start(bf16[8,1,8,256]{3,2,1,0:T(8,128)(2,1)} %bitcast.26), calls=%async_computation.1 | async-start | bytes 65536 | tf_op jit(solution)/shard_map/all_to_all | solution.py:129
  39.2 45.7 %reduce-scatter.5.cloned.1.call-start = ((), (), s32[]{:S(2)}) async-start(), calls=%async_computation.13 | async-start | bytes 589824 | tf_op jit(solution)/shard_map/reduce_scatter | solution.py:211
  89.2 9.2 %all-to-all-start.2 = ((f32[8,1,2048]{2,1,0:T(1,128)}), f32[8,1,2048]{2,1,0:T(1,128)S(1)}, u32[]{:S(2)}, u32[]{:S(2)}) async-start(f32[8,1,2048]{2,1,0:T(1,128)} %reshape.880), calls=%async_computation.3 | async-start | bytes 131072 | tf_op jit(solution)/shard_map/all_to_all | solution.py:218
  92.6 33.5 %all-reduce.6.cloned.1.call-start = ((), (), s32[]{:S(2)}) async-start(), calls=%async_computation.14 | async-start | bytes 131072 | tf_op jit(solution)/shard_map/psum | solution.py:222
  105.8 0.7 copy-start.31
  133.2 10.6 %all-to-all-start.3 = ((f32[8,1,2048]{2,1,0:T(1,128)}), f32[8,1,2048]{2,1,0:T(1,128)}, u32[]{:S(2)}, u32[]{:S(2)}) async-start(f32[8,1,2048]{2,1,0:T(1,128)} %reshape.882), calls=%async_computation.4 | async-start | bytes 131072 | tf_op jit(solution)/shard_map/all_to_all | solution.py:179
  137.8 80.9 %reduce-scatter.7.cloned.1.call-start = ((), (), s32[]{:S(2)}) async-start(), calls=%async_computation.15 | async-start | bytes 589824 | tf_op jit(solution)/shard_map/reduce_scatter | solution.py:211
  169.7 1.6 copy-start.10
  171.3 0.7 copy-start.9
  172.8 1.6 copy-start.10
  174.5 0.7 copy-start.9
  176.0 1.6 copy-start.10
  177.7 0.7 copy-start.9
  179.2 1.6 copy-start.10
  189.7 61.7 %all-reduce.8.cloned.1.call-start = ((), (), s32[]{:S(2)}) async-start(), calls=%async_computation.16 | async-start | bytes 131072 | tf_op jit(solution)/shard_map/psum | solution.py:222
  251.5 1.4 copy-start.15
  252.5 1.0 copy-start.5
  252.9 1.1 copy-start.2
  258.9 10.6 %all-to-all-start.5 = ((f32[8,1,2048]{2,1,0:T(1,128)}), f32[8,1,2048]{2,1,0:T(1,128)}, u32[]{:S(2)}, u32[]{:S(2)}) async-start(f32[8,1,2048]{2,1,0:T(1,128)} %reshape.886), calls=%async_computation.7 | async-start | bytes 131072 | tf_op jit(solution)/shard_map/all_to_all | solution.py:179
  263.5 81.0 %reduce-scatter.9.cloned.1.call-start = ((), (), s32[]{:S(2)}) async-start(), calls=%async_computation.17 | async-start | bytes 589824 | tf_op jit(solution)/shard_map/reduce_scatter | solution.py:211
  295.3 1.6 copy-start.12
  296.9 0.7 copy-start.11
  298.5 1.6 copy-start.12
  301.6 1.6 copy-start.12
  304.8 1.6 copy-start.12
  315.4 61.6 %all-reduce.10.cloned.1.call-start = ((), (), s32[]{:S(2)}) async-start(), calls=%async_computation.18 | async-start | bytes 131072 | tf_op jit(solution)/shard_map/psum | solution.py:222
  377.0 1.4 copy-start.16
  378.0 1.0 copy-start.6
  378.4 1.1 copy-start.3
  384.4 10.6 %all-to-all-start.7 = ((f32[8,1,2048]{2,1,0:T(1,128)}), f32[8,1,2048]{2,1,0:T(1,128)}, u32[]{:S(2)}, u32[]{:S(2)}) async-start(f32[8,1,2048]{2,1,0:T(1,128)} %reshape.890), calls=%async_computation.10 | async-start | bytes 131072 | tf_op jit(solution)/shard_map/all_to_all | solution.py:179
  389.0 81.0 %reduce-scatter.11.cloned.1.call-start = ((), (), s32[]{:S(2)}) async-start(), calls=%async_computation.19 | async-start | bytes 589824 | tf_op jit(solution)/shard_map/reduce_scatter | solution.py:211
  419.3 0.7 copy-start.7
  420.9 1.6 copy-start.8
  422.5 0.7 copy-start.7
  424.0 1.6 copy-start.8
  425.7 0.7 copy-start.7
  427.2 1.6 copy-start.8
  428.9 0.7 copy-start.7
  430.4 1.6 copy-start.8
  441.0 61.5 %all-reduce.12.cloned.1.call-start = ((), (), s32[]{:S(2)}) async-start(), calls=%async_computation.20 | async-start | bytes 131072 | tf_op jit(solution)/shard_map/psum | solution.py:222
  (20 other events, 13.5 us)
Sparse Core Ops, SparseCore 0:
  55.3 29.5 reduce-scatter.4
  106.6 19.3 all-reduce.5
  189.9 28.8 reduce-scatter.6
  231.9 19.5 all-reduce.7
  315.5 28.9 reduce-scatter.8
  357.6 19.3 all-reduce.9
  441.1 28.8 reduce-scatter.10
  483.1 19.3 all-reduce.11
where the time goes:
time: 516 us; the launch traced here: 512 us
  waiting for transfers between devices  215 us (42%)
  blocking collectives  78.2 us (15%)
  local copies, waits for them, and re-layouts  69.4 us (13%)
  matrix products  62 us (12%)
  other arithmetic  46.1 us (9%)
  starting transfers between devices  26.2 us (5%)
  between operations  15.1 us (3%)
    reduce_scatter x4, waiting for transfers between devices, local(): lax.psum_scatter(grid_term(jnp.int32(0), row_count * lax.axis_size(('tile...  111 us
    psum x4, waiting for transfers between devices, local(): gradient = lax.psum(conj_mul(coil_sens, coil_back), 'coil')  77.4 us
    all_gather x3, blocking collectives, local(): piece = lax.all_gather(kspace, ('tile', 'spk'), axis=0, tiled=True)  42.6 us
    dot_general x16, matrix products, grid_one_spoke(): jnp.dot(smeared.reshape(piece_rows * 2, RO), row_one, preferred_element_t...  29.2 us
    all_to_all x3, blocking collectives, local(): lax.all_to_all(partial_back, ('tile', 'spk'), split_axis=2, concat_axis=0...  24.9 us
    unnamed x82, local copies, waits for them, and re-layouts  24.4 us
    all_to_all x3, waiting for transfers between devices, local(): lax.all_to_all(half_done, ('tile', 'spk'), split_axis=2, concat_axis=0, t...  17.1 us
    dynamic_update_slice x12, other arithmetic, fold_one_spoke(): lax.dynamic_update_index_in_dim(partial_value, current + added, spoke_ind...  15.1 us
  transfers between devices with their start and end apart: 14, of which 13 were waited for; matrix products, arithmetic and copies ran while one was open for 3% of the time, Pallas kernels for 0%

commit v1 on v0

--- a/solution.py
+++ b/solution.py
@@ -12,6 +12,13 @@
 HIGH = lax.Precision.HIGHEST
 STEP_SIZE = 0.5
 RSQRT2 = 0.7071067811865476
+
+
+def exchange_blocks(shard, axis, split, join):
+    size = lax.axis_size(axis)
+    blocks = jnp.stack(jnp.split(shard, size, axis=split), axis=0)
+    blocks = lax.all_to_all(blocks, axis, split_axis=0, concat_axis=0)
+    return jnp.concatenate(blocks, axis=join)
 
 
 def dft_table(length, direction):
@@ -176,9 +183,7 @@
         else:
             coil_image = complex_mul(coil_sens, estimate)
             half_done = jnp.einsum("rpc,pcqv->rqv", coil_image, fwd_table, precision=HIGH)
-            turned = lax.all_to_all(
-                half_done, ("tile", "spk"), split_axis=2, concat_axis=0, tiled=True
-            )
+            turned = exchange_blocks(half_done, ("tile", "spk"), 2, 0)
             kspace = jnp.einsum("rpv,prqu->vqu", turned, fwd_table, precision=HIGH).astype(
                 jnp.bfloat16
             )

time: 516 us -> 511 us (level)
    all_to_all x6 -> x3, local copies, waits for them, and re-layouts: 10.5 us -> 5.35 us  [exchange_blocks(): blocks = lax.all_to_all(blocks, axis, split_axis=0, concat_axis=0)]
    unnamed x82 -> x112, local copies, waits for them, and re-layouts: 24.4 us -> 26.2 us
where the time goes in v1:
time: 511 us; the launch traced here: 508 us
  waiting for transfers between devices  215 us (42%)
  blocking collectives  78.4 us (15%)
  local copies, waits for them, and re-layouts  66.2 us (13%)
  matrix products  60.3 us (12%)
  other arithmetic  46 us (9%)
  starting transfers between devices  25.8 us (5%)
  between operations  15.2 us (3%)
    reduce_scatter x4, waiting for transfers between devices, local(): lax.psum_scatter(grid_term(jnp.int32(0), row_count * lax.axis_size(('tile...  112 us
    psum x4, waiting for transfers between devices, local(): gradient = lax.psum(conj_mul(coil_sens, coil_back), 'coil')  77.2 us
    all_gather x3, blocking collectives, local(): piece = lax.all_gather(kspace, ('tile', 'spk'), axis=0, tiled=True)  42.9 us
    dot_general x16, matrix products, grid_one_spoke(): jnp.dot(smeared.reshape(piece_rows * 2, RO), row_one, preferred_element_t...  29.3 us
    unnamed x112, local copies, waits for them, and re-layouts  26.2 us
    all_to_all x3, blocking collectives, local(): lax.all_to_all(partial_back, ('tile', 'spk'), split_axis=2, concat_axis=0...  24.9 us
    all_to_all x3, waiting for transfers between devices, exchange_blocks(): blocks = lax.all_to_all(blocks, axis, split_axis=0, concat_axis=0)  17.3 us
    dynamic_update_slice x12, other arithmetic, fold_one_spoke(): lax.dynamic_update_index_in_dim(partial_value, current + added, spoke_ind...  15.1 us
  transfers between devices with their start and end apart: 14, of which 13 were waited for; matrix products, arithmetic and copies ran while one was open for 3% of the time, Pallas kernels for 0%

profile of v1, /device:TPU:0, one launch (start us, length us, event | category | flops | bytes accessed | tf_op | source)
XLA Modules:
  0.0 507.7 jit_solution(15765767126400243369)
XLA Ops:
  8.6 10.6 %all-reduce = s32[8]{0:T(128)S(1)} all-reduce(s32[8]{0:T(128)S(1)} %dynamic-update-slice), channel_id=1, replica_groups=mesh['grp'=2,'tile'=4,'coil'=2,'spk'=2] {'tile','spk'}, use_global_device_ids=true, to_apply=%add | all-reduce | flops 8 | bytes 64
  22.0 3.3 all-to-all-start
  33.5 5.0 all-to-all-start.1
  39.2 5.1 %all-to-all-done.1 = bf16[8,1,8,256]{3,2,1,0:T(8,128)(2,1)S(1)} async-done(((bf16[8,1,8,256]{3,2,1,0:T(8,128)(2,1)}), bf16[8,1,8,256]{3,2,1,0:T(8,128)(2,1)S(1)}, u32[]{:S(2)}, u32[]{:S(2)}) %all-to-all-start.1) | async-done | bytes 32800 | tf_op jit(solution)/shard_map/all_to_all | solution.py:136
  47.0 7.6 %while.98 = (s32[]{:T(128)}, f32[256,2,256]{2,0,1:T(8,128)}, bf16[4,256,256]{2,1,0:T(8,128)(2,1)S(1)}, f32[4,2,256]{2,1,0:T(2,128)S(1)}, bf16[4,256,256]{2,1,0:T(8,128)(2,1)S(1)}, /*index=5*/s32[]{:T(128)}, s32[]{:T(128)}) while((s32[]{:T(128)}, f32[256,2,256]{2,0,1:T(8,128)}, bf16[4,256,256]{2,1,0:T(8,128)(2,1)S(1)}, ...), condition=%wide.region_3.4_spmd.clone, body=%wide.region_2.3_spmd.clone.sunk | while | flops 67698688 | bytes 1841251 | solution.py:173
  48.1 2.1 convolution_add_fusion.8
  50.3 2.1 convolution_add_fusion.8
  52.4 2.1 convolution_add_fusion.8
  56.4 2.6 select_select_fusion
  59.8 24.6 %reduce-scatter.5.cloned.1.call-done = f32[32,2,256]{2,0,1:T(8,128)} async-done(((f32[256,2,256]{2,0,1:T(8,128)}), f32[32,2,256]{2,0,1:T(8,128)}) %reduce-scatter.5.cloned.1.call-update) | async-done | bytes 65552 | tf_op jit(solution)/shard_map/reduce_scatter | solution.py:216
  88.7 3.4 all-to-all-start.2
  94.1 3.8 all-to-all-done.2
  106.8 18.6 %all-reduce.6.cloned.1.call-done = f32[32,2,256]{2,0,1:T(8,128)} async-done(((f32[32,2,256]{2,0,1:T(8,128)}), f32[32,2,256]{2,0,1:T(8,128)}) %all-reduce.6.cloned.1.call-update) | async-done | bytes 65552 | tf_op jit(solution)/shard_map/psum | solution.py:227
  131.4 4.6 all-to-all-start.3
  136.6 5.4 %all-to-all-done.3 = f32[8,1,2048]{2,1,0:T(1,128)} async-done(((f32[8,1,2048]{2,1,0:T(1,128)}), f32[8,1,2048]{2,1,0:T(1,128)}, u32[]{:S(2)}, u32[]{:S(2)}) %all-to-all-start.3) | async-done | bytes 65568 | tf_op jit(solution)/shard_map/all_to_all | solution.py:20
  142.0 2.3 reduce.1
  151.0 14.4 %all_gather.13 = bf16[256,2,256]{2,0,1:T(8,128)(2,1)S(1)} all-gather(bf16[32,2,256]{2,0,1:T(8,128)(2,1)S(1)} %fusion.32), channel_id=1, replica_groups=mesh['grp'=2,'tile'=4,'coil'=2,'spk'=2] {'tile','spk'}, dimensions={0}, use_global_device_ids=true | all-gather | bytes 294912 | tf_op jit(solution)/shard_map/all_gather | solution.py:190
  166.4 12.7 %while.95 = (s32[]{:T(128)}, f32[4,2,256]{2,1,0:T(2,128)}, bf16[4,256,256]{2,1,0:T(8,128)(2,1)S(1)}, bf16[512,256]{1,0:T(8,128)(2,1)S(1)}, bf16[4,256,256]{2,1,0:T(8,128)(2,1)S(1)}, /*index=5*/s32[]{:T(128)}) while((s32[]{:T(128)}, f32[4,2,256]{2,1,0:T(2,128)}, bf16[4,256,256]{2,1,0:T(8,128)(2,1)S(1)}, bf16[512,256]{1,0:T(8,128)(2,1)S(1)}, ...), condition=%wide.region_8.9_spmd, body=%wide.region_6.8_spmd.sunk | while | flops 67436544 | bytes 6300293 | solution.py:211
  180.4 7.5 %while.99 = (s32[]{:T(128)}, f32[256,2,256]{2,0,1:T(8,128)}, bf16[4,256,256]{2,1,0:T(8,128)(2,1)S(1)}, f32[4,2,256]{2,1,0:T(2,128)S(1)}, bf16[4,256,256]{2,1,0:T(8,128)(2,1)S(1)}, /*index=5*/s32[]{:T(128)}, s32[]{:T(128)}) while((s32[]{:T(128)}, f32[256,2,256]{2,0,1:T(8,128)}, bf16[4,256,256]{2,1,0:T(8,128)(2,1)S(1)}, ...), condition=%wide.region_10.11_spmd.clone, body=%wide.region_9.10_spmd.clone.sunk | while | flops 67698688 | bytes 1841251 | solution.py:173
  181.6 2.1 convolution_add_fusion.9
  183.7 2.1 convolution_add_fusion.9
  185.9 2.1 convolution_add_fusion.9
  188.0 29.0 %reduce-scatter.7.cloned.1.call-done = f32[32,2,256]{2,0,1:T(8,128)} async-done(((f32[256,2,256]{2,0,1:T(8,128)}), f32[32,2,256]{2,0,1:T(8,128)}) %reduce-scatter.7.cloned.1.call-update) | async-done | bytes 65552 | tf_op jit(solution)/shard_map/reduce_scatter | solution.py:216
  219.0 8.3 %all_to_all.97 = f32[8,1,2048]{2,1,0:T(1,128)S(1)} all-to-all(f32[8,1,2048]{2,1,0:T(1,128)S(1)} %reshape.896), channel_id=1, replica_groups=mesh['grp'=2,'tile'=4,'coil'=2,'spk'=2] {'tile','spk'}, dimensions={0} | all-to-all | bytes 131072 | tf_op jit(solution)/shard_map/all_to_all | solution.py:223
  230.1 19.5 %all-reduce.8.cloned.1.call-done = f32[32,2,256]{2,0,1:T(8,128)} async-done(((f32[32,2,256]{2,0,1:T(8,128)}), f32[32,2,256]{2,0,1:T(8,128)}) %all-reduce.8.cloned.1.call-update) | async-done | bytes 65552 | tf_op jit(solution)/shard_map/psum | solution.py:227
  255.8 4.6 all-to-all-start.5
  260.4 6.0 %all-to-all-done.5 = f32[8,1,2048]{2,1,0:T(1,128)} async-done(((f32[8,1,2048]{2,1,0:T(1,128)}), f32[8,1,2048]{2,1,0:T(1,128)}, u32[]{:S(2)}, u32[]{:S(2)}) %all-to-all-start.5) | async-done | bytes 65568 | tf_op jit(solution)/shard_map/all_to_all | solution.py:20
  266.4 2.3 reduce.3
  275.3 14.2 %all_gather.14 = bf16[256,2,256]{2,0,1:T(8,128)(2,1)S(1)} all-gather(bf16[32,2,256]{2,0,1:T(8,128)(2,1)S(1)} %fusion.33), channel_id=1, replica_groups=mesh['grp'=2,'tile'=4,'coil'=2,'spk'=2] {'tile','spk'}, dimensions={0}, use_global_device_ids=true | all-gather | bytes 294912 | tf_op jit(solution)/shard_map/all_gather | solution.py:190
  290.5 12.7 %while.96 = (s32[]{:T(128)}, f32[4,2,256]{2,1,0:T(2,128)}, bf16[4,256,256]{2,1,0:T(8,128)(2,1)S(1)}, bf16[512,256]{1,0:T(8,128)(2,1)S(1)}, bf16[4,256,256]{2,1,0:T(8,128)(2,1)S(1)}, /*index=5*/s32[]{:T(128)}) while((s32[]{:T(128)}, f32[4,2,256]{2,1,0:T(2,128)}, bf16[4,256,256]{2,1,0:T(8,128)(2,1)S(1)}, bf16[512,256]{1,0:T(8,128)(2,1)S(1)}, ...), condition=%wide.region_15.16_spmd, body=%wide.region_13.15_spmd.sunk | while | flops 67436544 | bytes 6300293 | solution.py:211
  304.6 7.5 %while.100 = (s32[]{:T(128)}, f32[256,2,256]{2,0,1:T(8,128)}, bf16[4,256,256]{2,1,0:T(8,128)(2,1)S(1)}, f32[4,2,256]{2,1,0:T(2,128)S(1)}, bf16[4,256,256]{2,1,0:T(8,128)(2,1)S(1)}, /*index=5*/s32[]{:T(128)}, s32[]{:T(128)}) while((s32[]{:T(128)}, f32[256,2,256]{2,0,1:T(8,128)}, bf16[4,256,256]{2,1,0:T(8,128)(2,1)S(1)}, ...), condition=%wide.region_17.18_spmd.clone, body=%wide.region_16.17_spmd.clone.sunk | while | flops 67698688 | bytes 1841251 | solution.py:173
  305.8 2.1 convolution_add_fusion.10
  307.9 2.1 convolution_add_fusion.10
  310.0 2.1 convolution_add_fusion.10
  312.2 28.9 %reduce-scatter.9.cloned.1.call-done = f32[32,2,256]{2,0,1:T(8,128)} async-done(((f32[256,2,256]{2,0,1:T(8,128)}), f32[32,2,256]{2,0,1:T(8,128)}) %reduce-scatter.9.cloned.1.call-update) | async-done | bytes 65552 | tf_op jit(solution)/shard_map/reduce_scatter | solution.py:216
  343.1 8.3 %all_to_all.98 = f32[8,1,2048]{2,1,0:T(1,128)S(1)} all-to-all(f32[8,1,2048]{2,1,0:T(1,128)S(1)} %reshape.900), channel_id=1, replica_groups=mesh['grp'=2,'tile'=4,'coil'=2,'spk'=2] {'tile','spk'}, dimensions={0} | all-to-all | bytes 131072 | tf_op jit(solution)/shard_map/all_to_all | solution.py:223
  354.2 19.5 %all-reduce.10.cloned.1.call-done = f32[32,2,256]{2,0,1:T(8,128)} async-done(((f32[32,2,256]{2,0,1:T(8,128)}), f32[32,2,256]{2,0,1:T(8,128)}) %all-reduce.10.cloned.1.call-update) | async-done | bytes 65552 | tf_op jit(solution)/shard_map/psum | solution.py:227
  379.9 4.6 all-to-all-start.7
  384.5 6.0 %all-to-all-done.7 = f32[8,1,2048]{2,1,0:T(1,128)} async-done(((f32[8,1,2048]{2,1,0:T(1,128)}), f32[8,1,2048]{2,1,0:T(1,128)}, u32[]{:S(2)}, u32[]{:S(2)}) %all-to-all-start.7) | async-done | bytes 65568 | tf_op jit(solution)/shard_map/all_to_all | solution.py:20
  390.5 2.3 reduce.5
  399.5 14.2 %all_gather.15 = bf16[256,2,256]{2,0,1:T(8,128)(2,1)S(1)} all-gather(bf16[32,2,256]{2,0,1:T(8,128)(2,1)S(1)} %fusion.34), channel_id=1, replica_groups=mesh['grp'=2,'tile'=4,'coil'=2,'spk'=2] {'tile','spk'}, dimensions={0}, use_global_device_ids=true | all-gather | bytes 294912 | tf_op jit(solution)/shard_map/all_gather | solution.py:190
  414.7 12.7 %while.97 = (s32[]{:T(128)}, f32[4,2,256]{2,1,0:T(2,128)}, bf16[4,256,256]{2,1,0:T(8,128)(2,1)S(1)}, bf16[512,256]{1,0:T(8,128)(2,1)S(1)}, bf16[4,256,256]{2,1,0:T(8,128)(2,1)S(1)}, /*index=5*/s32[]{:T(128)}) while((s32[]{:T(128)}, f32[4,2,256]{2,1,0:T(2,128)}, bf16[4,256,256]{2,1,0:T(8,128)(2,1)S(1)}, bf16[512,256]{1,0:T(8,128)(2,1)S(1)}, ...), condition=%wide.region_22.23_spmd, body=%wide.region_20.22_spmd.sunk | while | flops 67436544 | bytes 6300293 | solution.py:211
  428.8 7.5 %while.101 = (s32[]{:T(128)}, f32[256,2,256]{2,0,1:T(8,128)}, bf16[4,256,256]{2,1,0:T(8,128)(2,1)S(1)}, f32[4,2,256]{2,1,0:T(2,128)S(1)}, bf16[4,256,256]{2,1,0:T(8,128)(2,1)S(1)}, /*index=5*/s32[]{:T(128)}, s32[]{:T(128)}) while((s32[]{:T(128)}, f32[256,2,256]{2,0,1:T(8,128)}, bf16[4,256,256]{2,1,0:T(8,128)(2,1)S(1)}, ...), condition=%wide.region_24.25_spmd.clone, body=%wide.region_23.24_spmd.clone.sunk | while | flops 67698688 | bytes 1841251 | solution.py:173
  430.0 2.1 convolution_add_fusion.11
  434.2 2.1 convolution_add_fusion.11
  436.4 29.0 %reduce-scatter.11.cloned.1.call-done = f32[32,2,256]{2,0,1:T(8,128)} async-done(((f32[256,2,256]{2,0,1:T(8,128)}), f32[32,2,256]{2,0,1:T(8,128)}) %reduce-scatter.11.cloned.1.call-update) | async-done | bytes 65552 | tf_op jit(solution)/shard_map/reduce_scatter | solution.py:216
  467.3 8.3 %all_to_all.99 = f32[8,1,2048]{2,1,0:T(1,128)S(1)} all-to-all(f32[8,1,2048]{2,1,0:T(1,128)S(1)} %reshape.904), channel_id=1, replica_groups=mesh['grp'=2,'tile'=4,'coil'=2,'spk'=2] {'tile','spk'}, dimensions={0} | all-to-all | bytes 131072 | tf_op jit(solution)/shard_map/all_to_all | solution.py:223
  478.4 19.6 %all-reduce.12.cloned.1.call-done = f32[32,2,256]{2,0,1:T(8,128)} async-done(((f32[32,2,256]{2,0,1:T(8,128)}), f32[32,2,256]{2,0,1:T(8,128)}) %all-reduce.12.cloned.1.call-update) | async-done | bytes 65552 | tf_op jit(solution)/shard_map/psum | solution.py:227
  (435 shorter events, 140.5 us)
Async XLA Ops:
  6.5 14.3 %copy-start = (s32[8,256]{1,0:T(8,128)S(1)}, s32[8,256]{1,0:T(8,128)}, u32[]{:S(2)}) copy-start(s32[8,256]{1,0:T(8,128)} %param.23) | copy-start | bytes 24580
  22.0 11.5 %all-to-all-start = ((s32[8,1,256]{2,1,0:T(1,128)}), s32[8,1,256]{2,1,0:T(1,128)S(1)}, u32[]{:S(2)}, u32[]{:S(2)}) async-start(s32[8,1,256]{2,1,0:T(1,128)} %copy.109), calls=%async_computation | async-start | bytes 16384 | tf_op jit(solution)/shard_map/all_to_all | solution.py:139
  27.4 31.6 %copy-start.29 = (s32[8]{0:T(128)}, s32[8]{0:T(128)S(1)}, u32[]{:S(2)}) copy-start(s32[8]{0:T(128)S(1)} %get-tuple-element.881) | copy-start | bytes 100
  27.4 31.5 %copy-start.31 = (s32[8]{0:T(128)}, s32[8]{0:T(128)S(1)}, u32[]{:S(2)}) copy-start(s32[8]{0:T(128)S(1)} %get-tuple-element.882) | copy-start | bytes 100
  28.2 0.7 copy-start.22
  29.0 1.3 copy-start.26
  30.5 118.9 %copy-start.1 = (f32[1,256,2,256]{3,1,2,0:T(8,128)}, f32[1,256,2,256]{3,1,2,0:T(8,128)S(1)}, u32[]{:S(2)}) copy-start(f32[1,256,2,256]{3,1,2,0:T(8,128)S(1)} %get-tuple-element.830) | copy-start | bytes 1572868
  30.5 118.9 %copy-start.4 = (f32[1,256,2,256]{3,1,2,0:T(8,128)}, f32[1,256,2,256]{3,1,2,0:T(8,128)S(1)}, u32[]{:S(2)}) copy-start(f32[1,256,2,256]{3,1,2,0:T(8,128)S(1)} %get-tuple-element.833) | copy-start | bytes 1572868
  33.5 10.8 %all-to-all-start.1 = ((bf16[8,1,8,256]{3,2,1,0:T(8,128)(2,1)}), bf16[8,1,8,256]{3,2,1,0:T(8,128)(2,1)S(1)}, u32[]{:S(2)}, u32[]{:S(2)}) async-start(bf16[8,1,8,256]{3,2,1,0:T(8,128)(2,1)} %bitcast.26), calls=%async_computation.1 | async-start | bytes 65536 | tf_op jit(solution)/shard_map/all_to_all | solution.py:136
  38.5 45.9 %reduce-scatter.5.cloned.1.call-start = ((), (), s32[]{:S(2)}) async-start(), calls=%async_computation.13 | async-start | bytes 589824 | tf_op jit(solution)/shard_map/reduce_scatter | solution.py:216
  88.7 9.2 %all-to-all-start.2 = ((f32[8,1,2048]{2,1,0:T(1,128)}), f32[8,1,2048]{2,1,0:T(1,128)S(1)}, u32[]{:S(2)}, u32[]{:S(2)}) async-start(f32[8,1,2048]{2,1,0:T(1,128)} %reshape.892), calls=%async_computation.3 | async-start | bytes 131072 | tf_op jit(solution)/shard_map/all_to_all | solution.py:223
  92.0 33.4 %all-reduce.6.cloned.1.call-start = ((), (), s32[]{:S(2)}) async-start(), calls=%async_computation.14 | async-start | bytes 131072 | tf_op jit(solution)/shard_map/psum | solution.py:227
  105.2 0.7 copy-start.34
  128.9 0.7 copy-start.13
  131.4 10.6 %all-to-all-start.3 = ((f32[8,1,2048]{2,1,0:T(1,128)}), f32[8,1,2048]{2,1,0:T(1,128)}, u32[]{:S(2)}, u32[]{:S(2)}) async-start(f32[8,1,2048]{2,1,0:T(1,128)} %reshape.894), calls=%async_computation.4 | async-start | bytes 131072 | tf_op jit(solution)/shard_map/all_to_all | solution.py:20
  136.0 81.0 %reduce-scatter.7.cloned.1.call-start = ((), (), s32[]{:S(2)}) async-start(), calls=%async_computation.15 | async-start | bytes 589824 | tf_op jit(solution)/shard_map/reduce_scatter | solution.py:216
  167.9 1.6 copy-start.10
  171.1 1.6 copy-start.10
  174.2 1.6 copy-start.10
  177.4 1.6 copy-start.10
  188.0 61.6 %all-reduce.8.cloned.1.call-start = ((), (), s32[]{:S(2)}) async-start(), calls=%async_computation.16 | async-start | bytes 131072 | tf_op jit(solution)/shard_map/psum | solution.py:227
  249.6 1.4 copy-start.18
  250.6 1.0 copy-start.5
  251.0 1.1 copy-start.2
  253.3 0.7 copy-start.14
  255.8 10.6 %all-to-all-start.5 = ((f32[8,1,2048]{2,1,0:T(1,128)}), f32[8,1,2048]{2,1,0:T(1,128)}, u32[]{:S(2)}, u32[]{:S(2)}) async-start(f32[8,1,2048]{2,1,0:T(1,128)} %reshape.898), calls=%async_computation.7 | async-start | bytes 131072 | tf_op jit(solution)/shard_map/all_to_all | solution.py:20
  260.4 80.8 %reduce-scatter.9.cloned.1.call-start = ((), (), s32[]{:S(2)}) async-start(), calls=%async_computation.17 | async-start | bytes 589824 | tf_op jit(solution)/shard_map/reduce_scatter | solution.py:216
  292.1 1.6 copy-start.12
  295.2 1.6 copy-start.12
  298.4 1.6 copy-start.12
  300.0 0.7 copy-start.11
  301.6 1.6 copy-start.12
  312.2 61.5 %all-reduce.10.cloned.1.call-start = ((), (), s32[]{:S(2)}) async-start(), calls=%async_computation.18 | async-start | bytes 131072 | tf_op jit(solution)/shard_map/psum | solution.py:227
  373.7 1.4 copy-start.19
  374.8 1.0 copy-start.6
  375.1 1.1 copy-start.3
  377.4 0.7 copy-start.15
  379.9 10.6 %all-to-all-start.7 = ((f32[8,1,2048]{2,1,0:T(1,128)}), f32[8,1,2048]{2,1,0:T(1,128)}, u32[]{:S(2)}, u32[]{:S(2)}) async-start(f32[8,1,2048]{2,1,0:T(1,128)} %reshape.902), calls=%async_computation.10 | async-start | bytes 131072 | tf_op jit(solution)/shard_map/all_to_all | solution.py:20
  384.5 80.9 %reduce-scatter.11.cloned.1.call-start = ((), (), s32[]{:S(2)}) async-start(), calls=%async_computation.19 | async-start | bytes 589824 | tf_op jit(solution)/shard_map/reduce_scatter | solution.py:216
  414.7 0.7 copy-start.7
  416.2 1.6 copy-start.8
  417.9 0.7 copy-start.7
  419.4 1.6 copy-start.8
  421.1 0.7 copy-start.7
  422.6 1.6 copy-start.8
  424.2 0.7 copy-start.7
  425.8 1.6 copy-start.8
  436.3 61.6 %all-reduce.12.cloned.1.call-start = ((), (), s32[]{:S(2)}) async-start(), calls=%async_computation.20 | async-start | bytes 131072 | tf_op jit(solution)/shard_map/psum | solution.py:227
  (23 other events, 15.5 us)
Sparse Core Ops, SparseCore 0:
  54.7 29.6 reduce-scatter.4
  106.0 19.3 all-reduce.5
  188.1 28.8 reduce-scatter.6
  230.2 19.3 all-reduce.7
  312.3 28.8 reduce-scatter.8
  354.3 19.3 all-reduce.9
  436.4 28.8 reduce-scatter.10
  478.5 19.3 all-reduce.11
